TPU v7x, 256 devices: a whole 4x4x8 slice. The times are simulated.
256 devices in a mesh: row: 16 (over z, core), col: 16 (over y, x).
Axes of the slice: x: 4, y: 4, z: 8, core: 2. Of those that a mesh axis runs over, the one named last changes fastest.
Arguments:
- blocks: bfloat16 [16, 16, 5, 128, 8192], P('row', 'col'), may hold values from -6 to 6
- coords: int32 [16, 16, 5, 3], P('row', 'col'), may hold values from 0 to 15, as said below
- counts: int32 [16, 16], P('row', 'col'), may hold values from 1 to 5, as said below
- doc_factor: bfloat16 [32768, 128], P(('col', 'row')), may hold values from -6 to 6
- ctx_factor: bfloat16 [512, 128], P('col'), may hold values from -0.0625 to 0.0625
Outputs:
- mttkrp: float32 [32768, 128], P(('row', 'col'))
Inputs may be any that keep to these rules, and one draw needn't show every extreme that they name: coords[..., 0] lies in 0 to 15, coords[..., 1] in 0 to 15, coords[..., 2] in 0 to 7; slots at or past the device's count are ignored. `counts`: some device uses all 5 slots.
All inputs are finite; a program needn't handle non-finite values.
Results may differ from a plain program's by a relative error of at most 0.0029.
Values may be sent and summed in bfloat16 or wider, within the bound.
No kernel may reach another device: no remote copies, remote signals or barrier semaphores. Data moves between devices by JAX's collectives and lax.ppermute only.
A program may use at most 64 MiB of HBM per device.

v0:
```python
import jax
import jax.numpy as jnp
from jax import lax
from jax.experimental import pallas as pl
from jax.experimental.pallas import tpu as pltpu
from jax.sharding import PartitionSpec as P

BQ = 128
BD = 128
BK = 64
QBC = 1
DOC_CHUNK = 16
VMEM_LIMIT = 50 * 1024 * 1024


def gather_rows(piece, axis):
    copies = jnp.broadcast_to(piece[None], (lax.axis_size(axis),) + piece.shape)
    gathered = lax.all_to_all(copies, axis, 0, 0, tiled=True)
    return gathered.reshape(-1, piece.shape[-1])


def slot_kernel(coords_ref, count_ref, blocks_hbm, doc_ref, ctx_ref, out_ref, held, sems):
    n_doc = doc_ref.shape[0]
    n_ctx = ctx_ref.shape[0]
    n_q = out_ref.shape[0]
    slots = blocks_hbm.shape[0]
    pieces = held.shape[1]
    piece = held.shape[-1]
    used = jnp.clip(count_ref[0], 0, slots)

    def fetch(slot, part):
        return pltpu.make_async_copy(
            blocks_hbm.at[slot, :, pl.ds(part * piece, piece)],
            held.at[slot % 2, part],
            sems.at[slot % 2, part],
        )

    @pl.when(used > 0)
    def _():
        for part in range(pieces):
            fetch(0, part).start()

    out_ref[...] = jnp.zeros_like(out_ref)

    def step(slot, carry):
        @pl.when(slot + 1 < used)
        def _():
            for part in range(pieces):
                fetch(slot + 1, part).start()

        qid = jnp.clip(coords_ref[0, slot], 0, n_q - 1)
        did = jnp.clip(coords_ref[1, slot], 0, n_doc - 1)
        kid = jnp.clip(coords_ref[2, slot], 0, n_ctx - 1)
        crows = ctx_ref[kid]
        width = DOC_CHUNK * BK
        acc = jnp.zeros(out_ref.shape[1:], jnp.float32)
        for part in range(pieces):
            fetch(slot, part).wait()
            for sub in range(piece // width):
                first = (part * piece + sub * width) // BK
                brows = doc_ref[did, pl.ds(first, DOC_CHUNK), :]
                table = (brows[:, None, :] * crows[None, :, :]).reshape(width, crows.shape[-1])
                acc += jnp.dot(
                    held[slot % 2, part, :, pl.ds(sub * width, width)],
                    table,
                    preferred_element_type=jnp.float32,
                )
        out_ref[qid] += acc
        return carry

    lax.fori_loop(0, used, step, 0)


def slot_terms(own_blocks, own_coords, used, doc_blocks, ctx_blocks, n_q):
    slots, rows, width = own_blocks.shape
    rank = doc_blocks.shape[-1]
    pieces = 1
    cost = pl.CostEstimate(
        flops=2 * slots * rows * width * rank,
        bytes_accessed=own_blocks.size * 2 + n_q * rows * rank * 4,
        transcendentals=0,
    )
    return pl.pallas_call(
        slot_kernel,
        in_specs=[
            pl.BlockSpec(memory_space=pltpu.SMEM),
            pl.BlockSpec(memory_space=pltpu.SMEM),
            pl.BlockSpec(memory_space=pl.ANY),
            pl.BlockSpec(memory_space=pltpu.VMEM),
            pl.BlockSpec(memory_space=pltpu.VMEM),
        ],
        out_specs=pl.BlockSpec(memory_space=pltpu.VMEM),
        out_shape=jax.ShapeDtypeStruct((n_q, rows, rank), jnp.float32),
        scratch_shapes=[
            pltpu.VMEM((2, pieces, rows, width // pieces), own_blocks.dtype),
            pltpu.SemaphoreType.DMA((2, pieces)),
        ],
        compiler_params=pltpu.CompilerParams(vmem_limit_bytes=VMEM_LIMIT),
        cost_estimate=cost,
    )(own_coords.T, used.reshape(-1), own_blocks, doc_blocks, ctx_blocks)


def body(blocks, coords, counts, doc_factor, ctx_factor):
    doc_slab = lax.all_gather(doc_factor, "row", axis=0, tiled=True)
    ctx_all = gather_rows(ctx_factor, "col")
    rank = doc_slab.shape[1]
    n_q = QBC * lax.axis_size("col")
    doc_blocks = doc_slab.reshape(-1, BD, rank)
    ctx_blocks = ctx_all.reshape(-1, BK, rank)
    parts = slot_terms(blocks[0, 0], coords[0, 0], counts[0], doc_blocks, ctx_blocks, n_q)
    return lax.all_to_all(parts, "col", 0, 0, tiled=True).sum(axis=0)


def solution(mesh):
    placed = (
        P("row", "col", None, None, None),
        P("row", "col", None, None),
        P("row", "col"),
        P(("col", "row"), None),
        P("col", None),
    )
    return jax.shard_map(
        body, mesh=mesh, in_specs=placed, out_specs=P(("row", "col"), None), check_vma=False
    )
```

profile of v0, /device:TPU:1, one launch (start us, length us, event | category | flops | bytes accessed | tf_op | source)
XLA Modules:
  0.0 61.9 jit_solution(8997612582953396480)
XLA Ops:
  0.0 1.4 %broadcast_in_dim.2 = bf16[16,32,128]{2,1,0:T(8,128)(2,1)} broadcast(bf16[32,128]{1,0:T(8,128)(2,1)} %param.9), dimensions={1,2} | broadcast | bytes 139264 | tf_op jit(solution)/shard_map/broadcast_in_dim | solution.py:17
  1.4 7.6 %all-to-all-start = ((bf16[16,32,128]{2,1,0:T(8,128)(2,1)}), bf16[16,32,128]{2,1,0:T(8,128)(2,1)S(1)}, u32[]{:S(2)}, u32[]{:S(2)}) async-start(bf16[16,32,128]{2,1,0:T(8,128)(2,1)} %broadcast_in_dim.2), calls=%async_computation | async-start | bytes 262144 | tf_op jit(solution)/shard_map/all_to_all | solution.py:18
  8.9 22.4 %all_gather.3 = bf16[2048,128]{1,0:T(8,128)(2,1)S(1)} all-gather(bf16[128,128]{1,0:T(8,128)(2,1)} %param.8), channel_id=1, replica_groups=mesh['row'=16,'col'=16] {'row'}, dimensions={0}, use_global_device_ids=true | all-gather | bytes 557056 | tf_op jit(solution)/shard_map/all_gather | solution.py:104
  32.0 0.7 %copy.8 = s32[1,1,5,3]{2,3,1,0:T(4,128)S(1)} copy(s32[1,1,5,3]{2,1,3,0:T(1,128)} %param.6) | data formatting | bytes 120
  32.7 0.0 all-to-all-done
  32.7 7.5 %shard_map.55 = f32[16,128,128]{2,1,0:T(8,128)S(1)} custom-call(s32[3,5]{1,0:T(4,128)S(1)} %bitcast.12, s32[1]{0:T(128)} %bitcast.9.count_ref, bf16[5,128,8192]{2,1,0:T(8,128)(2,1)} %bitcast.13, bf16[16,128,128]{2,1,0:T(8,128)(2,1)S(1)} %bitcast.10, bf16[8,64,128]{2,1,0:T(8,128)(2,1)S(1)} %bitcast.11), custom_call_target="tpu_custom_call" | custom-call | flops 1342177280 | bytes 11534336 | tf_op jit(solution)/shard_map/pallas_call | solution.py:83
  40.3 21.0 %all_to_all.10 = f32[16,128,128]{2,1,0:T(8,128)S(1)} all-to-all(f32[16,128,128]{2,1,0:T(8,128)S(1)} %shard_map.55), channel_id=1, replica_groups=mesh['row'=16,'col'=16] {'col'}, dimensions={0} | all-to-all | bytes 2097152 | tf_op jit(solution)/shard_map/all_to_all | solution.py:111
  61.2 0.7 %reduce_sum.9 = f32[128,128]{1,0:T(8,128)} reduce(f32[16,128,128]{2,1,0:T(8,128)S(1)} %all_to_all.10, f32[]{:T(128)} %constant.0.clone.1), dimensions={0}, to_apply=%region_0.0 | reduce | flops 245760 | bytes 1114116 | tf_op jit(solution)/shard_map/reduce_sum | solution.py:111
Async XLA Ops:
  1.4 31.4 %all-to-all-start = ((bf16[16,32,128]{2,1,0:T(8,128)(2,1)}), bf16[16,32,128]{2,1,0:T(8,128)(2,1)S(1)}, u32[]{:S(2)}, u32[]{:S(2)}) async-start(bf16[16,32,128]{2,1,0:T(8,128)(2,1)} %broadcast_in_dim.2), calls=%async_computation | async-start | bytes 262144 | tf_op jit(solution)/shard_map/all_to_all | solution.py:18
where the time goes:
time: 62.9 us; the launch traced here: 61.9 us
  blocking collectives  43.4 us (69%)
  starting transfers between devices  7.57 us (12%)
  Pallas kernels  7.53 us (12%)
  local copies, waits for them, and re-layouts  2.03 us (3%)
  other arithmetic  0.69 us (1%)
  between operations  0.67 us (1%)
    all_gather x1, blocking collectives, body(): doc_slab = lax.all_gather(doc_factor, 'row', axis=0, tiled=True)  22.4 us
    all_to_all x1, blocking collectives, body(): return lax.all_to_all(parts, 'col', 0, 0, tiled=True).sum(axis=0)  21 us
    all_to_all x1, starting transfers between devices, gather_rows(): gathered = lax.all_to_all(copies, axis, 0, 0, tiled=True)  7.57 us
    pallas_call x1, Pallas kernels, slot_terms(): pl.pallas_call(slot_kernel, in_specs=[pl.BlockSpec(memory_space=pltpu.SME...  7.53 us
    broadcast_in_dim x1, local copies, waits for them, and re-layouts, gather_rows(): copies = jnp.broadcast_to(piece[None], (lax.axis_size(axis),) + piece.shape)  1.35 us
  transfers between devices with their start and end apart: 1, of which 0 were waited for; matrix products, arithmetic and copies ran while one was open for 1% of the time, Pallas kernels for 0%

commit v1 on v0

--- a/solution.py
+++ b/solution.py
@@ -24,14 +24,16 @@
     n_ctx = ctx_ref.shape[0]
     n_q = out_ref.shape[0]
     slots = blocks_hbm.shape[0]
-    pieces = held.shape[1]
-    piece = held.shape[-1]
+    total = held.shape[-1]
+    cuts = (0, total // 4, total)
+    pieces = len(cuts) - 1
     used = jnp.clip(count_ref[0], 0, slots)
 
     def fetch(slot, part):
+        span = pl.ds(cuts[part], cuts[part + 1] - cuts[part])
         return pltpu.make_async_copy(
-            blocks_hbm.at[slot, :, pl.ds(part * piece, piece)],
-            held.at[slot % 2, part],
+            blocks_hbm.at[slot, :, span],
+            held.at[slot % 2, :, span],
             sems.at[slot % 2, part],
         )
 
@@ -56,12 +58,11 @@
         acc = jnp.zeros(out_ref.shape[1:], jnp.float32)
         for part in range(pieces):
             fetch(slot, part).wait()
-            for sub in range(piece // width):
-                first = (part * piece + sub * width) // BK
-                brows = doc_ref[did, pl.ds(first, DOC_CHUNK), :]
+            for column in range(cuts[part], cuts[part + 1], width):
+                brows = doc_ref[did, pl.ds(column // BK, DOC_CHUNK), :]
                 table = (brows[:, None, :] * crows[None, :, :]).reshape(width, crows.shape[-1])
                 acc += jnp.dot(
-                    held[slot % 2, part, :, pl.ds(sub * width, width)],
+                    held[slot % 2, :, pl.ds(column, width)],
                     table,
                     preferred_element_type=jnp.float32,
                 )
@@ -74,7 +75,6 @@
 def slot_terms(own_blocks, own_coords, used, doc_blocks, ctx_blocks, n_q):
     slots, rows, width = own_blocks.shape
     rank = doc_blocks.shape[-1]
-    pieces = 1
     cost = pl.CostEstimate(
         flops=2 * slots * rows * width * rank,
         bytes_accessed=own_blocks.size * 2 + n_q * rows * rank * 4,
@@ -92,8 +92,8 @@
         out_specs=pl.BlockSpec(memory_space=pltpu.VMEM),
         out_shape=jax.ShapeDtypeStruct((n_q, rows, rank), jnp.float32),
         scratch_shapes=[
-            pltpu.VMEM((2, pieces, rows, width // pieces), own_blocks.dtype),
-            pltpu.SemaphoreType.DMA((2, pieces)),
+            pltpu.VMEM((2, rows, width), own_blocks.dtype),
+            pltpu.SemaphoreType.DMA((2, 2)),
         ],
         compiler_params=pltpu.CompilerParams(vmem_limit_bytes=VMEM_LIMIT),
         cost_estimate=cost,

time: 62.9 us -> 63.8 us (1.014); the launches traced: 61.9 us -> 63.6 us
  blocking collectives: 43.4 us -> 48.9 us
  Pallas kernels: 7.53 us -> 3.7 us
    all_to_all x1, blocking collectives: 21 us -> 26.5 us  [body(): return lax.all_to_all(parts, 'col', 0, 0, tiled=True).sum(axis=0)]
    pallas_call x1, Pallas kernels: 7.53 us -> 3.7 us  [slot_terms(): pl.pallas_call(slot_kernel, in_specs=[pl.BlockSpec(memory_space=pltpu.SME...]
where the time goes in v1:
time: 63.8 us; the launch traced here: 63.6 us
  blocking collectives  48.9 us (77%)
  starting transfers between devices  7.57 us (12%)
  Pallas kernels  3.7 us (6%)
  local copies, waits for them, and re-layouts  2.03 us (3%)
  other arithmetic  0.69 us (1%)
  between operations  0.67 us (1%)
    all_to_all x1, blocking collectives, body(): return lax.all_to_all(parts, 'col', 0, 0, tiled=True).sum(axis=0)  26.5 us
    all_gather x1, blocking collectives, body(): doc_slab = lax.all_gather(doc_factor, 'row', axis=0, tiled=True)  22.4 us
    all_to_all x1, starting transfers between devices, gather_rows(): gathered = lax.all_to_all(copies, axis, 0, 0, tiled=True)  7.57 us
    pallas_call x1, Pallas kernels, slot_terms(): pl.pallas_call(slot_kernel, in_specs=[pl.BlockSpec(memory_space=pltpu.SME...  3.7 us
    broadcast_in_dim x1, local copies, waits for them, and re-layouts, gather_rows(): copies = jnp.broadcast_to(piece[None], (lax.axis_size(axis),) + piece.shape)  1.35 us
  transfers between devices with their start and end apart: 1, of which 0 were waited for; matrix products, arithmetic and copies ran while one was open for 1% of the time, Pallas kernels for 0%

profile of v1, /device:TPU:1, one launch (start us, length us, event | category | flops | bytes accessed | tf_op | source)
XLA Modules:
  0.0 63.6 jit_solution(14960809711686128308)
XLA Ops:
  0.0 1.4 %broadcast_in_dim.2 = bf16[16,32,128]{2,1,0:T(8,128)(2,1)} broadcast(bf16[32,128]{1,0:T(8,128)(2,1)} %param.9), dimensions={1,2} | broadcast | bytes 139264 | tf_op jit(solution)/shard_map/broadcast_in_dim | solution.py:17
  1.4 7.6 %all-to-all-start = ((bf16[16,32,128]{2,1,0:T(8,128)(2,1)}), bf16[16,32,128]{2,1,0:T(8,128)(2,1)S(1)}, u32[]{:S(2)}, u32[]{:S(2)}) async-start(bf16[16,32,128]{2,1,0:T(8,128)(2,1)} %broadcast_in_dim.2), calls=%async_computation | async-start | bytes 262144 | tf_op jit(solution)/shard_map/all_to_all | solution.py:18
  8.9 22.4 %all_gather.3 = bf16[2048,128]{1,0:T(8,128)(2,1)S(1)} all-gather(bf16[128,128]{1,0:T(8,128)(2,1)} %param.8), channel_id=1, replica_groups=mesh['row'=16,'col'=16] {'row'}, dimensions={0}, use_global_device_ids=true | all-gather | bytes 557056 | tf_op jit(solution)/shard_map/all_gather | solution.py:104
  32.0 0.7 %copy.8 = s32[1,1,5,3]{2,3,1,0:T(4,128)S(1)} copy(s32[1,1,5,3]{2,1,3,0:T(1,128)} %param.6) | data formatting | bytes 120
  32.7 0.0 all-to-all-done
  32.7 3.7 %shard_map.55 = f32[16,128,128]{2,1,0:T(8,128)S(1)} custom-call(s32[3,5]{1,0:T(4,128)S(1)} %bitcast.12, s32[1]{0:T(128)} %bitcast.9.count_ref, bf16[5,128,8192]{2,1,0:T(8,128)(2,1)} %bitcast.13, bf16[16,128,128]{2,1,0:T(8,128)(2,1)S(1)} %bitcast.10, bf16[8,64,128]{2,1,0:T(8,128)(2,1)S(1)} %bitcast.11), custom_call_target="tpu_custom_call" | custom-call | flops 1342177280 | bytes 11534336 | tf_op jit(solution)/shard_map/pallas_call | solution.py:83
  36.4 26.5 %all_to_all.10 = f32[16,128,128]{2,1,0:T(8,128)S(1)} all-to-all(f32[16,128,128]{2,1,0:T(8,128)S(1)} %shard_map.55), channel_id=1, replica_groups=mesh['row'=16,'col'=16] {'col'}, dimensions={0} | all-to-all | bytes 2097152 | tf_op jit(solution)/shard_map/all_to_all | solution.py:111
  62.9 0.7 %reduce_sum.9 = f32[128,128]{1,0:T(8,128)} reduce(f32[16,128,128]{2,1,0:T(8,128)S(1)} %all_to_all.10, f32[]{:T(128)} %constant.0.clone.1), dimensions={0}, to_apply=%region_0.0 | reduce | flops 245760 | bytes 1114116 | tf_op jit(solution)/shard_map/reduce_sum | solution.py:111
Async XLA Ops:
  1.4 31.4 %all-to-all-start = ((bf16[16,32,128]{2,1,0:T(8,128)(2,1)}), bf16[16,32,128]{2,1,0:T(8,128)(2,1)S(1)}, u32[]{:S(2)}, u32[]{:S(2)}) async-start(bf16[16,32,128]{2,1,0:T(8,128)(2,1)} %broadcast_in_dim.2), calls=%async_computation | async-start | bytes 262144 | tf_op jit(solution)/shard_map/all_to_all | solution.py:18
